TPU v7x, 32 devices: a whole 2x2x4 slice. The times are simulated.
32 devices in a mesh: dp: 8 (over z, x), tensor: 4 (over y, core).
Axes of the slice: x: 2, y: 2, z: 4, core: 2. Of those that a mesh axis runs over, the one named last changes fastest.
Arguments:
- tokens: bfloat16 [16, 128, 2048], P('dp'), may hold values from -6 to 6
- cotangent: bfloat16 [16, 128, 2048], P('dp'), may hold values from -6 to 6
- routes: int32 [16, 128, 4], P('dp'), may hold values from 0 to 5, as said below
- gates: bfloat16 [16, 128, 4], P('dp'), may hold values from 0.099609375 to 0.5
- lengths: int32 [16], P('dp'), may hold values from 64 to 128, as said below
- deal: int32 [16], replicated, may hold values from 0 to 15, as said below
- norm1_gain: float32 [2048], P('dp'), may hold values from 0.1 to 1.9
- q_weight: float32 [2048, 2048], P('dp', 'tensor'), may hold values from -0.125 to 0.125
- q_bias: float32 [16, 128], P('tensor', 'dp'), may hold values from -3 to 3
- k_weight: float32 [2048, 2048], P('dp', 'tensor'), may hold values from -0.125 to 0.125
- v_weight: float32 [2048, 2048], P('dp', 'tensor'), may hold values from -0.125 to 0.125
- v_bias: float32 [16, 128], P('tensor', 'dp'), may hold values from -3 to 3
- o_weight: float32 [2048, 2048], P('tensor', 'dp'), may hold values from -0.75 to 0.75
- norm2_gain: float32 [2048], P('dp'), may hold values from 0.1 to 1.9
- expert_gate: float32 [6, 2048, 1408], P(None, 'dp', 'tensor'), may hold values from -0.125 to 0.125
- expert_up: float32 [6, 2048, 1408], P(None, 'dp', 'tensor'), may hold values from -0.125 to 0.125
- expert_down: float32 [6, 1408, 2048], P(None, 'tensor', 'dp'), may hold values from -0.21875 to 0.21875
- shared_gate: float32 [2048, 5632], P('dp', 'tensor'), may hold values from -0.125 to 0.125
- shared_up: float32 [2048, 5632], P('dp', 'tensor'), may hold values from -0.125 to 0.125
- shared_down: float32 [5632, 2048], P('tensor', 'dp'), may hold values from -0.109375 to 0.109375
- shared_switch: float32 [2048], P('dp'), may hold values from -0.125 to 0.125
Outputs:
- output: float32 [16, 128, 2048], P('dp', None, 'tensor')
- tokens_grad: float32 [16, 128, 2048], P('dp', None, 'tensor')
- norm1_gain_grad: float32 [2048], P('dp')
- q_weight_grad: float32 [2048, 2048], P('dp', 'tensor')
- q_bias_grad: float32 [16, 128], P('tensor', 'dp')
- k_weight_grad: float32 [2048, 2048], P('dp', 'tensor')
- v_weight_grad: float32 [2048, 2048], P('dp', 'tensor')
- v_bias_grad: float32 [16, 128], P('tensor', 'dp')
- o_weight_grad: float32 [2048, 2048], P('tensor', 'dp')
- norm2_gain_grad: float32 [2048], P('dp')
- expert_gate_grad: float32 [6, 2048, 1408], P(None, 'dp', 'tensor')
- expert_up_grad: float32 [6, 2048, 1408], P(None, 'dp', 'tensor')
- expert_down_grad: float32 [6, 1408, 2048], P(None, 'tensor', 'dp')
- shared_gate_grad: float32 [2048, 5632], P('dp', 'tensor')
- shared_up_grad: float32 [2048, 5632], P('dp', 'tensor')
- shared_down_grad: float32 [5632, 2048], P('tensor', 'dp')
- shared_switch_grad: float32 [2048], P('dp')
Inputs may be any that keep to these rules, and one draw needn't show every extreme that they name: Sequences 2i and 2i+1 are given on dp index i. The two sequences dealt to one dp index have lengths adding up to exactly 192. `deal`: dealt slot 2i holds sequence 2i; the odd sequences move by one common rotation of the dp indices: slot 2i+1 holds sequence 2((i - r) mod the number of dp indices) + 1, for one r of the draw. `routes`: each row names 4 different experts. Among the 192 real tokens dealt to one dp index, every expert is named by exactly 128 tokens. Rows past a sequence's length hold valid ids too.
All inputs are finite; a program needn't handle non-finite values.
Results may differ from a plain program's by a relative error of at most 0.013.
The roundings to bfloat16 on the way count: a program that leaves them out, or rounds other values in their place, can miss the bound.
Values may be sent and summed in bfloat16 or wider, within the bound.
A program may use at most 256 MiB of HBM per device.

v0:
```python
from functools import partial
import jax
import jax.numpy as jnp
from jax import lax
from jax.sharding import PartitionSpec as P

HEAD_DIM = 128
EPSILON = 1e-06
NEGATIVE = -1e30
LANES = 128
BF16 = jnp.bfloat16
F32 = jnp.float32
ALL = ("dp", "tensor")


def normalize(values, gain):
    return values * lax.rsqrt(jnp.mean(values * values, axis=-1, keepdims=True) + EPSILON) * gain


def nt(left, right):
    return lax.dot_general(left, right, (((1,), (1,)), ((), ())), preferred_element_type=F32)


def tn(left, right):
    return lax.dot_general(left, right, (((0,), (0,)), ((), ())), preferred_element_type=F32)


def nn(left, right):
    return lax.dot_general(left, right, (((1,), (0,)), ((), ())), preferred_element_type=F32)


def gather_all(value):
    return lax.all_gather(value, ALL, axis=0, tiled=True)


def scatter_all(value):
    return lax.psum_scatter(value, ALL, scatter_dimension=0, tiled=True)


def exchange_dp(value):
    return lax.all_to_all(value, "dp", 0, 0, tiled=False)


def per_device(
    tokens,
    cotangent,
    routes,
    gates,
    lengths,
    deal,
    norm1_gain,
    q_weight,
    q_bias,
    k_weight,
    v_weight,
    v_bias,
    o_weight,
    norm2_gain,
    expert_gate,
    expert_up,
    expert_down,
    shared_gate,
    shared_up,
    shared_down,
    shared_switch,
):
    n_dp = lax.axis_size("dp")
    n_tensor = lax.axis_size("tensor")
    place = lax.axis_index("dp")
    member = lax.axis_index("tensor")
    seqs, span, width = tokens.shape
    rows = seqs * span
    shard = rows // n_tensor
    experts, slice_d, expert_cols = expert_gate.shape
    shared_cols = shared_gate.shape[1]
    head_cols = q_weight.shape[1]
    heads = head_cols // HEAD_DIM

    def own_rows(value):
        return lax.dynamic_slice_in_dim(value, member * shard, shard, 0)

    valid = (jnp.arange(span)[None, :] < lengths[:, None]).reshape(rows, 1)
    dense = jnp.zeros((seqs, span, LANES), F32)
    for rank in range(routes.shape[-1]):
        hit = routes[..., rank, None] == jnp.arange(LANES)
        dense = dense + jnp.where(hit, gates[..., rank, None].astype(F32), 0.0)
    dense = dense.reshape(rows, LANES).astype(BF16)
    cot = jnp.where(valid, cotangent.reshape(rows, width), 0).astype(BF16)
    cot_packed = gather_all(own_rows(jnp.concatenate([cot, dense], axis=1)))
    small = jnp.concatenate(
        [norm1_gain, norm2_gain, shared_switch, q_bias.reshape(-1), v_bias.reshape(-1)]
    ).astype(BF16)
    small = lax.all_gather(small[None, :], "dp", axis=0, tiled=True)
    gain_one = small[:, :slice_d].reshape(-1).astype(F32)
    gain_two = small[:, slice_d : 2 * slice_d].reshape(-1).astype(F32)
    switch = small[:, 2 * slice_d : 3 * slice_d].reshape(1, -1)
    piece = q_bias.shape[1]

    def whole_bias(start):
        part = small[:, start : start + heads * piece].reshape(n_dp, heads, piece)
        return part.transpose(1, 0, 2).reshape(-1).astype(F32)

    bias_q = whole_bias(3 * slice_d)
    bias_v = whole_bias(3 * slice_d + heads * piece)
    attn_weights = jnp.concatenate(
        [
            q_weight.astype(BF16),
            k_weight.astype(BF16),
            v_weight.astype(BF16),
            o_weight.T.astype(BF16),
        ],
        axis=1,
    )
    attn_weights = lax.all_gather(attn_weights, "dp", axis=0, tiled=True)
    weight_qkv = attn_weights[:, : 3 * head_cols]
    weight_o = attn_weights[:, 3 * head_cols :]

    def by_unit(expert_part, shared_part):
        return jnp.concatenate(
            [
                expert_part.astype(BF16).reshape(n_dp, -1, slice_d),
                shared_part.astype(BF16).reshape(n_dp, -1, slice_d),
            ],
            axis=1,
        )

    gate_sent = by_unit(
        expert_gate.astype(BF16).transpose(0, 2, 1).reshape(-1, slice_d), shared_gate.astype(BF16).T
    )
    up_sent = by_unit(
        expert_up.astype(BF16).transpose(0, 2, 1).reshape(-1, slice_d), shared_up.astype(BF16).T
    )
    down_sent = by_unit(expert_down.reshape(-1, slice_d), shared_down)
    arrived = exchange_dp(jnp.stack([gate_sent, up_sent, down_sent], axis=1))
    units = arrived.shape[2]
    routed = experts * expert_cols // n_dp
    arrived = arrived.transpose(1, 2, 0, 3).reshape(3, units, width)
    gate_units, up_units, down_units = (arrived[0], arrived[1], arrived[2])
    inputs = tokens.reshape(rows, width).astype(F32)
    inputs_own = own_rows(inputs)
    normed_one = normalize(inputs, gain_one).astype(BF16)
    projected = nn(normed_one, weight_qkv)
    head_shape = (seqs, span, heads, HEAD_DIM)
    queries = (projected[:, :head_cols] + bias_q).astype(BF16).reshape(head_shape)
    keys = projected[:, head_cols : 2 * head_cols].astype(BF16).reshape(head_shape)
    values = (projected[:, 2 * head_cols :] + bias_v).astype(BF16).reshape(head_shape)
    order = jnp.arange(span)
    causal = order[None, :] <= order[:, None]
    scale = HEAD_DIM ** (-0.5)
    scores = jnp.einsum("bqhd,bkhd->bhqk", queries, keys, preferred_element_type=F32) * scale
    scores = jnp.where(causal, scores, NEGATIVE)
    top = jnp.max(scores, axis=-1, keepdims=True)
    powers = jnp.exp(scores - top)
    probs = powers / jnp.sum(powers, axis=-1, keepdims=True)
    probs_low = probs.astype(BF16)
    attended = (
        jnp.einsum("bhqk,bkhd->bqhd", probs_low, values, preferred_element_type=F32)
        .reshape(rows, -1)
        .astype(BF16)
    )
    attn_part = nt(attended, weight_o)
    middle = inputs_own + lax.psum_scatter(attn_part, "tensor", scatter_dimension=0, tiled=True)
    normed_two = gather_all(normalize(middle, gain_two).astype(BF16))
    cot_all = cot_packed[:, :width]
    route_share = cot_packed[:, width : width + LANES]
    unit_expert = (place * routed + jnp.arange(routed)) // expert_cols
    picks = (jnp.arange(LANES)[:, None] == unit_expert[None, :]).astype(BF16)
    gate_logit = nt(normed_two, switch)
    switch_gate = jax.nn.sigmoid(gate_logit)
    share = jnp.concatenate(
        [
            nn(route_share, picks),
            jnp.broadcast_to(switch_gate, (switch_gate.shape[0], units - routed)),
        ],
        axis=1,
    )
    gate_act = nt(normed_two, gate_units)
    up_act = nt(normed_two, up_units)
    logistic = jax.nn.sigmoid(gate_act)
    silu = gate_act * logistic
    inner = (silu * up_act).astype(BF16).astype(F32)
    inner_share = (inner * share).astype(BF16)
    mixed = nn(inner_share, down_units).astype(BF16)
    mixed = lax.psum_scatter(mixed, "dp", scatter_dimension=0, tiled=True)
    mixed = lax.psum_scatter(mixed, "tensor", scatter_dimension=1, tiled=True)
    grad_inner_raw = nt(cot_all, down_units)
    grad_logit = (
        jnp.sum(inner[:, routed:] * grad_inner_raw[:, routed:], axis=1, keepdims=True)
        * switch_gate
        * (1.0 - switch_gate)
    )
    grad_inner = grad_inner_raw * share
    slope = logistic * (1.0 + gate_act * (1.0 - logistic))
    grad_gate_act = (grad_inner * up_act * slope).astype(BF16)
    grad_up_act = (grad_inner * silu).astype(BF16)
    back_two = nn(grad_gate_act, gate_units) + nn(grad_up_act, up_units)
    back_two = (back_two + grad_logit * switch.astype(F32)).astype(BF16)
    back_two = scatter_all(back_two).astype(F32)
    grad_down = tn(inner_share, cot_all)
    grad_gate = tn(grad_gate_act, normed_two)
    grad_up = tn(grad_up_act, normed_two)
    grad_switch = jnp.sum(grad_logit * normed_two.astype(F32), axis=0)
    sent_back = jnp.stack([grad_gate, grad_up, grad_down]).astype(BF16)
    sent_back = sent_back.reshape(3, units, n_dp, slice_d).transpose(2, 0, 1, 3)
    returned = exchange_dp(sent_back).astype(F32)

    def split_units(value):
        routed_part = value[:, :routed].reshape(experts, expert_cols, slice_d)
        return (routed_part, value[:, routed:].reshape(shared_cols, slice_d))

    grad_gate_experts, grad_gate_shared = split_units(returned[:, 0])
    grad_up_experts, grad_up_shared = split_units(returned[:, 1])
    grad_down_experts, grad_down_shared = split_units(returned[:, 2])
    unused_two, norm_two_back = jax.vjp(normalize, middle, gain_two)
    grad_middle_norm, grad_gain_two = norm_two_back(back_two)
    grad_middle = own_rows(cot).astype(F32) + grad_middle_norm
    grad_attn = lax.all_gather(grad_middle.astype(BF16), "tensor", axis=0, tiled=True)
    grad_weight_o = tn(grad_attn, attended)
    grad_attended = nn(grad_attn, weight_o).astype(BF16).reshape(head_shape)
    grad_values = (
        jnp.einsum("bhqk,bqhd->bkhd", probs_low, grad_attended, preferred_element_type=F32)
        .astype(BF16)
        .reshape(rows, -1)
    )
    grad_probs = jnp.einsum("bqhd,bkhd->bhqk", grad_attended, values, preferred_element_type=F32)
    grad_scores = (
        probs * (grad_probs - jnp.sum(grad_probs * probs, axis=-1, keepdims=True))
    ).astype(BF16)
    grad_queries = (
        (jnp.einsum("bhqk,bkhd->bqhd", grad_scores, keys, preferred_element_type=F32) * scale)
        .astype(BF16)
        .reshape(rows, -1)
    )
    grad_keys = (
        (jnp.einsum("bhqk,bqhd->bkhd", grad_scores, queries, preferred_element_type=F32) * scale)
        .astype(BF16)
        .reshape(rows, -1)
    )
    grad_qkv = jnp.concatenate([grad_queries, grad_keys, grad_values], axis=1)
    grad_attn_weights = jnp.concatenate([tn(normed_one, grad_qkv), grad_weight_o], axis=1).astype(
        BF16
    )
    grad_attn_weights = lax.psum_scatter(
        grad_attn_weights, "dp", scatter_dimension=0, tiled=True
    ).astype(F32)
    back_one = nt(grad_qkv, weight_qkv)
    back_one = lax.psum_scatter(back_one, "tensor", scatter_dimension=0, tiled=True)
    unused_one, norm_one_back = jax.vjp(normalize, inputs_own, gain_one)
    grad_input_norm, grad_gain_one = norm_one_back(back_one)
    grad_input = grad_middle + grad_input_norm
    bias_part = jnp.concatenate(
        [
            jnp.sum(grad_queries.astype(F32), axis=0).reshape(heads, n_dp, piece),
            jnp.sum(grad_values.astype(F32), axis=0).reshape(heads, n_dp, piece),
        ],
        axis=0,
    )
    bias_part = bias_part.transpose(1, 0, 2).reshape(1, n_dp, -1)
    mine = (jnp.arange(n_tensor) == member)[:, None, None]
    bias_part = jnp.where(mine, bias_part, 0.0)
    gains = jnp.concatenate([grad_gain_one, grad_gain_two, grad_switch])
    gains = gains.reshape(1, 3, n_dp, slice_d).transpose(0, 2, 1, 3).reshape(n_dp, 3 * slice_d)
    pack = jnp.concatenate([gains, bias_part.transpose(1, 0, 2).reshape(n_dp, -1)], axis=1)
    pack = lax.psum(pack, ALL)
    pack = lax.dynamic_slice_in_dim(pack, place, 1, 0)[0]
    bias_own = lax.dynamic_slice_in_dim(
        pack[3 * slice_d :].reshape(n_tensor, 2, heads, piece), member, 1, 0
    )[0]

    def to_columns(value):
        return lax.all_to_all(value, "tensor", 1, 0, tiled=True)

    out_shape = (seqs, span, width // n_tensor)
    output = jnp.where(valid, to_columns(middle) + mixed.astype(F32), 0.0).reshape(out_shape)
    tokens_grad = jnp.where(valid, to_columns(grad_input), 0.0).reshape(out_shape)
    return (
        output,
        tokens_grad,
        pack[:slice_d],
        grad_attn_weights[:, :head_cols],
        bias_own[0],
        grad_attn_weights[:, head_cols : 2 * head_cols],
        grad_attn_weights[:, 2 * head_cols : 3 * head_cols],
        bias_own[1],
        grad_attn_weights[:, 3 * head_cols :].T,
        pack[slice_d : 2 * slice_d],
        grad_gate_experts.transpose(0, 2, 1),
        grad_up_experts.transpose(0, 2, 1),
        grad_down_experts,
        grad_gate_shared.T,
        grad_up_shared.T,
        grad_down_shared,
        pack[2 * slice_d : 3 * slice_d],
    )


IN_SPECS = (
    P("dp", None, None),
    P("dp", None, None),
    P("dp", None, None),
    P("dp", None, None),
    P("dp"),
    P(),
    P("dp"),
    P("dp", "tensor"),
    P("tensor", "dp"),
    P("dp", "tensor"),
    P("dp", "tensor"),
    P("tensor", "dp"),
    P("tensor", "dp"),
    P("dp"),
    P(None, "dp", "tensor"),
    P(None, "dp", "tensor"),
    P(None, "tensor", "dp"),
    P("dp", "tensor"),
    P("dp", "tensor"),
    P("tensor", "dp"),
    P("dp"),
)
OUT_SPECS = (P("dp", None, "tensor"), P("dp", None, "tensor")) + IN_SPECS[6:]


def solution(mesh):
    return jax.shard_map(
        per_device, mesh=mesh, in_specs=IN_SPECS, out_specs=OUT_SPECS, check_vma=False
    )
```

profile of v0, /device:TPU:0, one launch (start us, length us, event | category | flops | bytes accessed | tf_op | source)
XLA Modules:
  0.0 1104.9 jit_solution(10503144483082694511)
XLA Ops:
  13.3 33.5 %all-gather = bf16[8,1,896]{2,1,0:T(2,128)(2,1)S(1)} all-gather(bf16[1,1,896]{2,1,0:T(2,128)(2,1)S(1)} %bitcast.258), channel_id=1, replica_groups=mesh['dp'=8,'tensor'=4] {'dp'}, dimensions={0}, use_global_device_ids=true | all-gather | bytes 16128 | tf_op jit(solution)/shard_map/all_gather | solution.py:93
  49.2 91.7 %all-gather.6.cloned.1.call-done = bf16[2048,2048]{0,1:T(8,128)(2,1)} async-done(((bf16[256,2048]{0,1:T(8,128)(2,1)}), bf16[2048,2048]{0,1:T(8,128)(2,1)}) %all-gather.6.cloned.1.call-update) | async-done | bytes 8388624 | tf_op jit(solution)/shard_map/all_gather | solution.py:114
  140.9 4.6 fusion.7
  149.5 3.6 fusion.18
  156.4 26.3 %reduce-scatter.7.cloned.1.call-done = f32[64,2048]{1,0:T(8,128)} async-done(((f32[256,2048]{1,0:T(8,128)}), f32[64,2048]{1,0:T(8,128)}) %reduce-scatter.7.cloned.1.call-update) | async-done | bytes 524304 | tf_op jit(solution)/shard_map/reduce_scatter | solution.py:162
  200.5 5.5 all-to-all-start.1
  206.3 145.4 %all-to-all-done.1 = bf16[8,3,440,256]{3,2,1,0:T(8,128)(2,1)} async-done(((bf16[8,3,440,256]{3,2,1,0:T(8,128)(2,1)}), bf16[8,3,440,256]{3,2,1,0:T(8,128)(2,1)}, u32[]{:S(2)}, u32[]{:S(2)}) %all-to-all-start.1) | async-done | bytes 5406752 | tf_op jit(solution)/shard_map/all_to_all | solution.py:41
  361.9 44.5 %all-gather.8.cloned.1.call-done = bf16[2048,2048]{1,0:T(8,128)(2,1)} async-done(((bf16[64,2048]{1,0:T(8,128)(2,1)}), bf16[2048,2048]{1,0:T(8,128)(2,1)}) %all-gather.8.cloned.1.call-update) | async-done | bytes 8388624 | tf_op jit(solution)/shard_map/all_gather | solution.py:33
  406.4 5.8 fusion.73
  412.6 5.7 fusion.72
  418.3 5.8 fusion.71
  424.3 11.5 %multiply_convert_fusion = (bf16[2048,440]{0,1:T(8,128)(2,1)}, bf16[2048,440]{0,1:T(8,128)(2,1)S(1)}, bf16[2048,440]{0,1:T(8,128)(2,1)}, f32[2048,440]{0,1:T(8,128)}, f32[2048,440]{0,1:T(8,128)}) fusion(f32[2048,176]{0,1:T(8,128)S(1)} %broadcast_in_dim.169, f32[2048,264]{0,1:T(8,128)S(1)} %copy-done.11, f32[2048,440]{0,1:T(8,128)} %fusion.71, ...), kind=kOutput, calls=%fused_computation.24 | convolution fusion | flops 3709009920 | bytes 33619968 | tf_op jit(solution)/shard_map/dot_general | solution.py:21
  438.5 8.2 fusion.74
  446.6 11.2 %add_convert_fusion = bf16[2048,2048]{1,0:T(8,128)(2,1)} fusion(f32[2048,2048]{1,0:T(8,128)} %fusion.74, f32[2048]{0:T(1024)S(1)} %convert_element_type.270, f32[2048]{0:T(1024)S(1)} %subtract_multiply_fusion, bf16[2048,440]{0,1:T(8,128)(2,1)} %get-tuple-element.98, bf16[440,2048]{1,0:T(8,128)(2,1)S(1)} %bitcast.231), kind=kOutput, calls=%fused_computation.2 | convolution fusion | flops 3707764736 | bytes 28786688 | tf_op jit(solution)/shard_map/dot_general | solution.py:29
  458.4 9.9 convolution_convert_fusion.1
  468.3 138.6 %reduce-scatter.13.cloned.1.call-done = bf16[64,2048]{1,0:T(8,128)(2,1)} async-done(((bf16[2048,2048]{1,0:T(8,128)(2,1)}), bf16[64,2048]{1,0:T(8,128)(2,1)}) %reduce-scatter.13.cloned.1.call-update) | async-done | bytes 262160 | tf_op jit(solution)/shard_map/reduce_scatter | solution.py:37
  610.1 143.7 %reduce-scatter.9.cloned.1.call-done = bf16[256,2048]{1,0:T(8,128)(2,1)} async-done(((bf16[2048,2048]{1,0:T(8,128)(2,1)}), bf16[256,2048]{1,0:T(8,128)(2,1)}) %reduce-scatter.9.cloned.1.call-update) | async-done | bytes 1048592 | tf_op jit(solution)/shard_map/reduce_scatter | solution.py:184
  753.8 3.4 fusion.25
  767.8 6.2 fusion.5
  777.6 4.5 convolution_convert_fusion
  782.2 8.4 pad_maximum_fusion
  790.6 7.8 fusion.13
  800.8 7.5 convolution_convert_fusion.4
  810.3 4.1 convolution_convert_fusion.3
  818.3 4.9 all-to-all-start.3
  824.1 5.1 multiply_reduce_fusion
  829.2 179.2 %all-to-all-done.3 = bf16[8,3,440,256]{3,2,1,0:T(8,128)(2,1)} async-done(((bf16[8,3,440,256]{3,2,1,0:T(8,128)(2,1)}), bf16[8,3,440,256]{3,2,1,0:T(8,128)(2,1)}, u32[]{:S(2)}, u32[]{:S(2)}) %all-to-all-start.3) | async-done | bytes 5406752 | tf_op jit(solution)/shard_map/all_to_all | solution.py:41
  1008.4 3.5 all-to-all-start
  1011.9 3.5 copy_convert_fusion
  1015.4 4.2 slice_bitcast_fusion
  1044.7 3.5 all-to-all-start.2
  1048.2 41.3 %psum.7 = f32[8,1280]{1,0:T(8,128)S(1)} all-reduce(f32[8,1280]{1,0:T(8,128)S(1)} %pad_maximum_fusion.4), channel_id=1, replica_groups=mesh['dp'=8,'tensor'=4] {'dp','tensor'}, use_global_device_ids=true, to_apply=%region_19.20 | all-reduce | flops 10240 | bytes 81920 | tf_op jit(solution)/shard_map/psum | solution.py:264
  (244 shorter events, 105.4 us)
Async XLA Ops:
  8.0 132.9 %all-gather.6.cloned.1.call-start = ((), (), s32[]{:S(2)}) async-start(), calls=%async_computation.10 | async-start | bytes 9437184 | tf_op jit(solution)/shard_map/all_gather | solution.py:114
  11.7 35.6 %copy-start.4 = (bf16[2,128,2048]{2,1,0:T(8,128)(2,1)S(1)}, bf16[2,128,2048]{2,1,0:T(8,128)(2,1)}, u32[]{:S(2)}) copy-start(bf16[2,128,2048]{2,1,0:T(8,128)(2,1)} %param.21) | copy-start | bytes 3145732
  12.8 169.9 %reduce-scatter.7.cloned.1.call-start = ((), (), s32[]{:S(2)}) async-start(), calls=%async_computation.11 | async-start | bytes 2621440 | tf_op jit(solution)/shard_map/reduce_scatter | solution.py:162
  148.0 5.2 copy-start.12
  149.5 3.8 copy-start.36
  149.5 4.3 copy-start.25
  149.5 4.3 copy-start.26
  153.2 205.8 %all-gather.10.cloned.1.call-start = ((), (), s32[]{:S(2)}) async-start(), calls=%async_computation.13 | async-start | bytes 9191424 | tf_op jit(solution)/shard_map/all_gather | solution.py:33
  153.8 28.9 %copy-start.27 = (pred[256]{0:T(512)(128)(4,1)}, pred[256]{0:T(512)(128)(4,1)S(1)}, u32[]{:S(2)}) copy-start(pred[256]{0:T(512)(128)(4,1)S(1)} %get-tuple-element.131) | copy-start | bytes 772
  156.4 250.0 %all-gather.8.cloned.1.call-start = ((), (), s32[]{:S(2)}) async-start(), calls=%async_computation.12 | async-start | bytes 8650752 | tf_op jit(solution)/shard_map/all_gather | solution.py:33
  200.5 151.3 %all-to-all-start.1 = ((bf16[8,3,440,256]{3,2,1,0:T(8,128)(2,1)}), bf16[8,3,440,256]{3,2,1,0:T(8,128)(2,1)}, u32[]{:S(2)}, u32[]{:S(2)}) async-start(bf16[8,3,440,256]{3,2,1,0:T(8,128)(2,1)} %pad_maximum_fusion.1), calls=%async_computation.2 | async-start | bytes 10813440 | tf_op jit(solution)/shard_map/all_to_all | solution.py:41
  206.0 400.9 %reduce-scatter.13.cloned.1.call-start = ((), (), s32[]{:S(2)}) async-start(), calls=%async_computation.16 | async-start | bytes 8650752 | tf_op jit(solution)/shard_map/reduce_scatter | solution.py:37
  406.4 5.8 copy-start
  406.4 6.3 copy-start.15
  412.6 5.7 copy-start.16
  418.3 6.0 copy-start.11
  418.3 6.0 copy-start.14
  435.8 10.8 copy-start.37
  457.9 295.8 %reduce-scatter.9.cloned.1.call-start = ((), (), s32[]{:S(2)}) async-start(), calls=%async_computation.14 | async-start | bytes 9437184 | tf_op jit(solution)/shard_map/reduce_scatter | solution.py:184
  468.3 285.6 %all-gather.12.cloned.1.call-start = ((), (), s32[]{:S(2)}) async-start(), calls=%async_computation.17 | async-start | bytes 1310720 | tf_op jit(solution)/shard_map/all_gather | solution.py:217
  610.0 428.9 %reduce-scatter.11.cloned.1.call-start = ((), (), s32[]{:S(2)}) async-start(), calls=%async_computation.15 | async-start | bytes 1310720 | tf_op jit(solution)/shard_map/reduce_scatter | solution.py:185
  753.8 287.0 %reduce-scatter.15.cloned.1.call-start = ((), (), s32[]{:S(2)}) async-start(), calls=%async_computation.18 | async-start | bytes 2621440 | tf_op jit(solution)/shard_map/reduce_scatter | solution.py:247
  774.0 317.8 %reduce-scatter.17.cloned.1.call-start = ((), (), s32[]{:S(2)}) async-start(), calls=%async_computation.19 | async-start | bytes 9437184 | tf_op jit(solution)/shard_map/reduce_scatter | solution.py:243
  798.4 10.8 slice-start
  800.8 8.4 slice-start.1
  818.3 5.8 copy-start.31
  818.3 190.1 %all-to-all-start.3 = ((bf16[8,3,440,256]{3,2,1,0:T(8,128)(2,1)}), bf16[8,3,440,256]{3,2,1,0:T(8,128)(2,1)}, u32[]{:S(2)}, u32[]{:S(2)}) async-start(bf16[8,3,440,256]{3,2,1,0:T(8,128)(2,1)} %maximum_bitcast_fusion), calls=%async_computation.9 | async-start | bytes 10813440 | tf_op jit(solution)/shard_map/all_to_all | solution.py:41
  1008.4 30.5 %all-to-all-start = ((f32[64,4,512]{2,0,1:T(8,128)}), f32[64,4,512]{2,0,1:T(8,128)S(1)}, u32[]{:S(2)}, u32[]{:S(2)}) async-start(f32[64,4,512]{2,0,1:T(8,128)} %bitcast.197), calls=%async_computation.1 | async-start | bytes 1048576 | tf_op jit(solution)/shard_map/all_to_all | solution.py:271
  1035.6 5.2 copy-start.24
  1035.6 6.7 copy-start.7
  1042.3 48.6 %copy-start.32 = (pred[2,128]{1,0:T(4,128)(4,1)S(1)}, pred[2,128]{1,0:T(4,128)(4,1)}, u32[]{:S(2)}) copy-start(pred[2,128]{1,0:T(4,128)(4,1)} %get-tuple-element.130) | copy-start | bytes 772
  1044.7 46.2 %all-to-all-start.2 = ((f32[64,4,512]{2,0,1:T(8,128)}), f32[64,4,512]{2,0,1:T(8,128)S(1)}, u32[]{:S(2)}, u32[]{:S(2)}) async-start(f32[64,4,512]{2,0,1:T(8,128)} %bitcast.196), calls=%async_computation.7 | async-start | bytes 1048576 | tf_op jit(solution)/shard_map/all_to_all | solution.py:271
  (24 other events, 49.3 us)
Sparse Core Ops, SparseCore 0:
  13.0 127.8 all-gather.5
  153.3 29.3 reduce-scatter.6
  610.1 12.5 all-gather.11
  753.9 23.8 reduce-scatter.10
  780.2 31.1 reduce-scatter.14
  814.9 251.4 reduce-scatter.16
Sparse Core Ops, SparseCore 1:
  157.1 113.9 all-gather.9
  274.4 131.9 all-gather.7
  458.0 148.8 reduce-scatter.12
  610.5 143.2 reduce-scatter.8
where the time goes:
time: 1110 us; the launch traced here: 1100 us
  waiting for transfers between devices  770 us (69%)
  matrix products  111 us (10%)
  blocking collectives  74.8 us (7%)
  local copies, waits for them, and re-layouts  66.3 us (6%)
  other arithmetic  47.6 us (4%)
  starting transfers between devices  18.5 us (2%)
  between operations  16.9 us (2%)
    all_to_all x2, waiting for transfers between devices, exchange_dp(): return lax.all_to_all(value, 'dp', 0, 0, tiled=False)  325 us
    reduce_scatter x1, waiting for transfers between devices, per_device(): mixed = lax.psum_scatter(mixed, 'dp', scatter_dimension=0, tiled=True)  144 us
    reduce_scatter x1, waiting for transfers between devices, scatter_all(): return lax.psum_scatter(value, ALL, scatter_dimension=0, tiled=True)  139 us
    all_gather x1, waiting for transfers between devices, per_device(): attn_weights = lax.all_gather(attn_weights, 'dp', axis=0, tiled=True)  91.7 us
    all_gather x2, waiting for transfers between devices, gather_all(): return lax.all_gather(value, ALL, axis=0, tiled=True)  44.5 us
    psum x1, blocking collectives, per_device(): pack = lax.psum(pack, ALL)  41.3 us
    dot_general x6, matrix products, nn(): lax.dot_general(left, right, (((1,), (0,)), ((), ())), preferred_element_...  40.1 us
    dot_general x6, matrix products, nt(): lax.dot_general(left, right, (((1,), (1,)), ((), ())), preferred_element_...  38.7 us
  transfers between devices with their start and end apart: 14, of which 7 were waited for; matrix products, arithmetic and copies ran while one was open for 13% of the time, Pallas kernels for 0%

commit v1 on v0

--- a/solution.py
+++ b/solution.py
@@ -11,6 +11,29 @@
 BF16 = jnp.bfloat16
 F32 = jnp.float32
 ALL = ("dp", "tensor")
+
+
+def _detail_links(q_in, dev_axis):
+    z = lax.axis_size(dev_axis)
+    part_now = lax.axis_index(dev_axis)
+    parts_out, s_next, ready = (z, part_now, q_in.shape[0])
+    log = tuple(((j, (j + 1) % parts_out) for j in range(parts_out)))
+    sides = tuple(((j, (j - 1) % parts_out) for j in range(parts_out)))
+    main = jnp.zeros((*q_in.shape[:0], parts_out * ready, *q_in.shape[1:]), q_in.dtype)
+    main = lax.dynamic_update_slice_in_dim(main, q_in, s_next * ready, axis=0)
+    b_now = y_new = q_in
+    front = parts_out // 2
+    for no in [*range(1, front + 1)]:
+        b_now = lax.ppermute(b_now, dev_axis, log)
+        main = lax.dynamic_update_slice_in_dim(
+            main, b_now, (s_next - no) % parts_out * ready, axis=0
+        )
+        if no < parts_out - front:
+            y_new = lax.ppermute(y_new, dev_axis, sides)
+            main = lax.dynamic_update_slice_in_dim(
+                main, y_new, (s_next + no) % parts_out * ready, axis=0
+            )
+    return main
 
 
 def normalize(values, gain):
@@ -111,7 +134,7 @@
         ],
         axis=1,
     )
-    attn_weights = lax.all_gather(attn_weights, "dp", axis=0, tiled=True)
+    attn_weights = _detail_links(attn_weights, "dp")
     weight_qkv = attn_weights[:, : 3 * head_cols]
     weight_o = attn_weights[:, 3 * head_cols :]
 

time: 1110 us -> 1180 us (1.063)
  waiting for transfers between devices: 770 us -> 793 us
  blocking collectives: 74.8 us -> 90.4 us
  starting transfers between devices: 18.5 us -> 31.4 us
    ppermute x0 -> x7, waiting for transfers between devices: none -> 115 us  [the longest x4 76.3 us: _detail_links(): b_now = lax.ppermute(b_now, dev_axis, log)]
    all_gather x1 -> x0, waiting for transfers between devices: 91.7 us -> none  [per_device(): attn_weights = lax.all_gather(attn_weights, 'dp', axis=0, tiled=True)]
    all_gather x1, blocking collectives: 33.5 us -> 48.8 us  [per_device(): small = lax.all_gather(small[None, :], 'dp', axis=0, tiled=True)]
    ppermute x0 -> x7, starting transfers between devices: none -> 13.1 us  [the longest x4 8 us: _detail_links(): b_now = lax.ppermute(b_now, dev_axis, log)]
  transfers between devices with their start and end apart: 14 -> 20, of which waited for: 7 -> 10; matrix products, arithmetic and copies ran while one was open for 13% -> 13% of each run, Pallas kernels for 0% -> 0%
where the time goes in v1:
time: 1180 us; the launch traced here: 1170 us
  waiting for transfers between devices  793 us (67%)
  matrix products  111 us (9%)
  blocking collectives  90.4 us (8%)
  local copies, waits for them, and re-layouts  76.5 us (6%)
  other arithmetic  50.4 us (4%)
  starting transfers between devices  31.4 us (3%)
  between operations  16.8 us (1%)
    all_to_all x2, waiting for transfers between devices, exchange_dp(): return lax.all_to_all(value, 'dp', 0, 0, tiled=False)  326 us
    reduce_scatter x1, waiting for transfers between devices, per_device(): mixed = lax.psum_scatter(mixed, 'dp', scatter_dimension=0, tiled=True)  144 us
    reduce_scatter x1, waiting for transfers between devices, scatter_all(): return lax.psum_scatter(value, ALL, scatter_dimension=0, tiled=True)  139 us
    ppermute x4, waiting for transfers between devices, _detail_links(): b_now = lax.ppermute(b_now, dev_axis, log)  76.3 us
    all_gather x1, blocking collectives, per_device(): small = lax.all_gather(small[None, :], 'dp', axis=0, tiled=True)  48.8 us
    all_gather x2, waiting for transfers between devices, gather_all(): return lax.all_gather(value, ALL, axis=0, tiled=True)  44.5 us
    psum x1, blocking collectives, per_device(): pack = lax.psum(pack, ALL)  41.6 us
    dot_general x6, matrix products, nn(): lax.dot_general(left, right, (((1,), (0,)), ((), ())), preferred_element_...  40.2 us
  transfers between devices with their start and end apart: 20, of which 10 were waited for; matrix products, arithmetic and copies ran while one was open for 13% of the time, Pallas kernels for 0%

profile of v1, /device:TPU:0, one launch (start us, length us, event | category | flops | bytes accessed | tf_op | source)
XLA Modules:
  0.0 1170.1 jit_solution(388563664363587503)
XLA Ops:
  12.7 4.4 broadcast_in_dim.155
  24.6 42.2 %collective-permute-done = bf16[256,2048]{0,1:T(8,128)(2,1)S(1)} collective-permute-done((bf16[256,2048]{0,1:T(8,128)(2,1)}, bf16[256,2048]{0,1:T(8,128)(2,1)S(1)}, u32[]{:S(2)}, u32[]{:S(2)}) %collective-permute-start) | collective-permute-done | bytes 1048608 | tf_op jit(solution)/shard_map/ppermute | solution.py:27
  69.6 48.8 %all-gather = bf16[8,1,896]{2,1,0:T(2,128)(2,1)S(1)} all-gather(bf16[1,1,896]{2,1,0:T(2,128)(2,1)S(1)} %bitcast.258), channel_id=1, replica_groups=mesh['dp'=8,'tensor'=4] {'dp'}, dimensions={0}, use_global_device_ids=true | all-gather | bytes 16128 | tf_op jit(solution)/shard_map/all_gather | solution.py:116
  122.9 38.2 %collective-permute-done.3 = bf16[256,2048]{0,1:T(8,128)(2,1)} collective-permute-done((bf16[256,2048]{0,1:T(8,128)(2,1)S(1)}, bf16[256,2048]{0,1:T(8,128)(2,1)}, u32[]{:S(2)}, u32[]{:S(2)}) %collective-permute-start.3) | collective-permute-done | bytes 1048608 | tf_op jit(solution)/shard_map/ppermute | solution.py:32
  162.4 16.6 %collective-permute-done.4 = bf16[256,2048]{0,1:T(8,128)(2,1)S(1)} collective-permute-done((bf16[256,2048]{0,1:T(8,128)(2,1)}, bf16[256,2048]{0,1:T(8,128)(2,1)S(1)}, u32[]{:S(2)}, u32[]{:S(2)}) %collective-permute-start.4) | collective-permute-done | bytes 1048608 | tf_op jit(solution)/shard_map/ppermute | solution.py:27
  189.3 17.5 %collective-permute-done.6 = bf16[256,2048]{0,1:T(8,128)(2,1)S(1)} collective-permute-done((bf16[256,2048]{0,1:T(8,128)(2,1)S(1)}, bf16[256,2048]{0,1:T(8,128)(2,1)S(1)}, u32[]{:S(2)}, u32[]{:S(2)}) %collective-permute-start.6) | collective-permute-done | bytes 1048608 | tf_op jit(solution)/shard_map/ppermute | solution.py:27
  207.9 4.6 fusion.7
  216.6 3.6 fusion.18
  223.5 25.4 %reduce-scatter.7.cloned.1.call-done = f32[64,2048]{1,0:T(8,128)} async-done(((f32[256,2048]{1,0:T(8,128)}), f32[64,2048]{1,0:T(8,128)}) %reduce-scatter.7.cloned.1.call-update) | async-done | bytes 524304 | tf_op jit(solution)/shard_map/reduce_scatter | solution.py:185
  265.0 5.5 all-to-all-start.1
  270.8 147.0 %all-to-all-done.1 = bf16[8,3,440,256]{3,2,1,0:T(8,128)(2,1)} async-done(((bf16[8,3,440,256]{3,2,1,0:T(8,128)(2,1)}), bf16[8,3,440,256]{3,2,1,0:T(8,128)(2,1)}, u32[]{:S(2)}, u32[]{:S(2)}) %all-to-all-start.1) | async-done | bytes 5406752 | tf_op jit(solution)/shard_map/all_to_all | solution.py:64
  428.0 44.5 %all-gather.5.cloned.1.call-done = bf16[2048,2048]{1,0:T(8,128)(2,1)} async-done(((bf16[64,2048]{1,0:T(8,128)(2,1)}), bf16[2048,2048]{1,0:T(8,128)(2,1)}) %all-gather.5.cloned.1.call-update) | async-done | bytes 8388624 | tf_op jit(solution)/shard_map/all_gather | solution.py:56
  472.5 5.8 fusion.75
  478.7 5.8 fusion.74
  484.6 5.8 fusion.73
  490.5 11.7 %multiply_convert_fusion = (bf16[2048,440]{0,1:T(8,128)(2,1)}, bf16[2048,440]{0,1:T(8,128)(2,1)S(1)}, bf16[2048,440]{0,1:T(8,128)(2,1)}, f32[2048,440]{0,1:T(8,128)}, f32[2048,440]{0,1:T(8,128)}) fusion(f32[2048,176]{0,1:T(8,128)S(1)} %broadcast_in_dim.173, f32[2048,264]{0,1:T(8,128)S(1)} %copy-done.11, f32[2048,440]{0,1:T(8,128)} %fusion.73, ...), kind=kOutput, calls=%fused_computation.24 | convolution fusion | flops 3709009920 | bytes 33619968 | tf_op jit(solution)/shard_map/dot_general | solution.py:44
  504.8 8.2 fusion.76
  513.0 11.2 add_convert_fusion
  524.5 9.9 convolution_convert_fusion.1
  534.5 138.8 %reduce-scatter.13.cloned.1.call-done = bf16[64,2048]{1,0:T(8,128)(2,1)} async-done(((bf16[2048,2048]{1,0:T(8,128)(2,1)}), bf16[64,2048]{1,0:T(8,128)(2,1)}) %reduce-scatter.13.cloned.1.call-update) | async-done | bytes 262160 | tf_op jit(solution)/shard_map/reduce_scatter | solution.py:60
  676.5 143.7 %reduce-scatter.9.cloned.1.call-done = bf16[256,2048]{1,0:T(8,128)(2,1)} async-done(((bf16[2048,2048]{1,0:T(8,128)(2,1)}), bf16[256,2048]{1,0:T(8,128)(2,1)}) %reduce-scatter.9.cloned.1.call-update) | async-done | bytes 1048592 | tf_op jit(solution)/shard_map/reduce_scatter | solution.py:207
  835.2 6.0 fusion.5
  844.8 4.5 convolution_convert_fusion
  849.4 8.7 pad_maximum_fusion
  858.1 7.8 fusion.13
  867.4 7.6 convolution_convert_fusion.4
  876.5 4.1 convolution_convert_fusion.3
  884.6 4.9 all-to-all-start.3
  890.4 5.1 multiply_reduce_fusion
  895.4 179.3 %all-to-all-done.3 = bf16[8,3,440,256]{3,2,1,0:T(8,128)(2,1)} async-done(((bf16[8,3,440,256]{3,2,1,0:T(8,128)(2,1)}), bf16[8,3,440,256]{3,2,1,0:T(8,128)(2,1)}, u32[]{:S(2)}, u32[]{:S(2)}) %all-to-all-start.3) | async-done | bytes 5406752 | tf_op jit(solution)/shard_map/all_to_all | solution.py:64
  1081.7 4.2 slice_bitcast_fusion
  1113.1 41.6 %psum.7 = f32[8,1280]{1,0:T(8,128)S(1)} all-reduce(f32[8,1280]{1,0:T(8,128)S(1)} %pad_maximum_fusion.4), channel_id=1, replica_groups=mesh['dp'=8,'tensor'=4] {'dp','tensor'}, use_global_device_ids=true, to_apply=%region_19.20 | all-reduce | flops 10240 | bytes 81920 | tf_op jit(solution)/shard_map/psum | solution.py:287
  (263 shorter events, 140.3 us)
Async XLA Ops:
  8.0 240.8 %reduce-scatter.7.cloned.1.call-start = ((), (), s32[]{:S(2)}) async-start(), calls=%async_computation.10 | async-start | bytes 2621440 | tf_op jit(solution)/shard_map/reduce_scatter | solution.py:185
  12.7 56.5 %copy-start.33 = (f32[256]{0:T(256)S(1)}, f32[256]{0:T(256)}, u32[]{:S(2)}) copy-start(f32[256]{0:T(256)} %param.26) | copy-start | bytes 3076
  12.7 56.5 %copy-start.34 = (f32[256]{0:T(256)S(1)}, f32[256]{0:T(256)}, u32[]{:S(2)}) copy-start(f32[256]{0:T(256)} %param.33) | copy-start | bytes 3076
  12.7 56.6 %copy-start.35 = (f32[256]{0:T(256)S(1)}, f32[256]{0:T(256)}, u32[]{:S(2)}) copy-start(f32[256]{0:T(256)} %param.40) | copy-start | bytes 3076
  12.7 56.6 %copy-start.29 = (f32[4,16]{1,0:T(4,128)S(1)}, f32[4,16]{1,0:T(4,128)}, u32[]{:S(2)}) copy-start(f32[4,16]{1,0:T(4,128)} %param.28) | copy-start | bytes 772
  12.7 56.7 %copy-start.30 = (f32[4,16]{1,0:T(4,128)S(1)}, f32[4,16]{1,0:T(4,128)}, u32[]{:S(2)}) copy-start(f32[4,16]{1,0:T(4,128)} %param.31) | copy-start | bytes 772
  17.1 103.6 %copy-start.4 = (bf16[2,128,2048]{2,1,0:T(8,128)(2,1)S(1)}, bf16[2,128,2048]{2,1,0:T(8,128)(2,1)}, u32[]{:S(2)}) copy-start(bf16[2,128,2048]{2,1,0:T(8,128)(2,1)} %param.21) | copy-start | bytes 3145732
  18.6 48.2 %collective-permute-start = (bf16[256,2048]{0,1:T(8,128)(2,1)}, bf16[256,2048]{0,1:T(8,128)(2,1)S(1)}, u32[]{:S(2)}, u32[]{:S(2)}) collective-permute-start(bf16[256,2048]{0,1:T(8,128)(2,1)} %get-tuple-element.111), channel_id=1, source_target_pairs={{0,4},{4,8},{8,12},{12,16},{16,20},{20,24},{24,28},{28,0},{1,5},{5... | collective-permute-start | bytes 3145736 | tf_op jit(solution)/shard_map/ppermute | solution.py:27
  21.6 96.8 %collective-permute-start.1 = (bf16[256,2048]{0,1:T(8,128)(2,1)}, bf16[256,2048]{0,1:T(8,128)(2,1)S(1)}, u32[]{:S(2)}, u32[]{:S(2)}) collective-permute-start(bf16[256,2048]{0,1:T(8,128)(2,1)} %get-tuple-element.111), channel_id=1, source_target_pairs={{0,28},{4,0},{8,4},{12,8},{16,12},{20,16},{24,20},{28,24},{1,29},{... | collective-permute-start | bytes 3145736 | tf_op jit(solution)/shard_map/ppermute | solution.py:32
  66.8 54.5 %copy-start.18 = (bf16[256,2048]{0,1:T(8,128)(2,1)}, bf16[256,2048]{0,1:T(8,128)(2,1)S(1)}, u32[]{:S(2)}) copy-start(bf16[256,2048]{0,1:T(8,128)(2,1)S(1)} %collective-permute-done) | copy-start | bytes 3145732
  66.8 54.2 %collective-permute-start.2 = (bf16[256,2048]{0,1:T(8,128)(2,1)S(1)}, bf16[256,2048]{0,1:T(8,128)(2,1)}, u32[]{:S(2)}, u32[]{:S(2)}) collective-permute-start(bf16[256,2048]{0,1:T(8,128)(2,1)S(1)} %collective-permute-done), channel_id=1, source_target_pairs={{0,4},{4,8},{8,12},{12,16},{16,20},{20,24},{24,28},{28,0},{1,5},{5... | collective-permute-start | bytes 3145736 | tf_op jit(solution)/shard_map/ppermute | solution.py:27
  118.4 42.7 %collective-permute-start.3 = (bf16[256,2048]{0,1:T(8,128)(2,1)S(1)}, bf16[256,2048]{0,1:T(8,128)(2,1)}, u32[]{:S(2)}, u32[]{:S(2)}) collective-permute-start(bf16[256,2048]{0,1:T(8,128)(2,1)S(1)} %collective-permute-done.1), channel_id=1, source_target_pairs={{0,28},{4,0},{8,4},{12,8},{16,12},{20,16},{24,20},{28,24},{1,29},{... | collective-permute-start | bytes 3145736 | tf_op jit(solution)/shard_map/ppermute | solution.py:32
  120.4 42.0 %copy-start.23 = (f32[1,2,8,128]{3,1,2,0:T(2,128)}, f32[1,2,8,128]{3,1,2,0:T(2,128)S(1)}, u32[]{:S(2)}) copy-start(f32[1,2,8,128]{3,1,2,0:T(2,128)S(1)} %copy.189) | copy-start | bytes 24580
  121.0 57.9 %collective-permute-start.4 = (bf16[256,2048]{0,1:T(8,128)(2,1)}, bf16[256,2048]{0,1:T(8,128)(2,1)S(1)}, u32[]{:S(2)}, u32[]{:S(2)}) collective-permute-start(bf16[256,2048]{0,1:T(8,128)(2,1)} %collective-permute-done.2), channel_id=1, source_target_pairs={{0,4},{4,8},{8,12},{12,16},{16,20},{20,24},{24,28},{28,0},{1,5},{5... | collective-permute-start | bytes 3145736 | tf_op jit(solution)/shard_map/ppermute | solution.py:27
  121.3 40.0 %copy-start.19 = (bf16[256,2048]{0,1:T(8,128)(2,1)S(1)}, bf16[256,2048]{0,1:T(8,128)(2,1)}, u32[]{:S(2)}) copy-start(bf16[256,2048]{0,1:T(8,128)(2,1)} %copy-done.18) | copy-start | bytes 3145732
  161.1 27.1 %collective-permute-start.5 = (bf16[256,2048]{0,1:T(8,128)(2,1)}, bf16[256,2048]{0,1:T(8,128)(2,1)S(1)}, u32[]{:S(2)}, u32[]{:S(2)}) collective-permute-start(bf16[256,2048]{0,1:T(8,128)(2,1)} %collective-permute-done.3), channel_id=1, source_target_pairs={{0,28},{4,0},{8,4},{12,8},{16,12},{20,16},{24,20},{28,24},{1,29},{... | collective-permute-start | bytes 3145736 | tf_op jit(solution)/shard_map/ppermute | solution.py:32
  179.0 27.8 %collective-permute-start.6 = (bf16[256,2048]{0,1:T(8,128)(2,1)S(1)}, bf16[256,2048]{0,1:T(8,128)(2,1)S(1)}, u32[]{:S(2)}, u32[]{:S(2)}) collective-permute-start(bf16[256,2048]{0,1:T(8,128)(2,1)S(1)} %collective-permute-done.4), channel_id=1, source_target_pairs={{0,4},{4,8},{8,12},{12,16},{16,20},{20,24},{24,28},{28,0},{1,5},{5... | collective-permute-start | bytes 3145736 | tf_op jit(solution)/shard_map/ppermute | solution.py:27
  220.2 204.9 %all-gather.7.cloned.1.call-start = ((), (), s32[]{:S(2)}) async-start(), calls=%async_computation.12 | async-start | bytes 9191424 | tf_op jit(solution)/shard_map/all_gather | solution.py:56
  220.9 33.2 %copy-start.27 = (pred[256]{0:T(512)(128)(4,1)}, pred[256]{0:T(512)(128)(4,1)S(1)}, u32[]{:S(2)}) copy-start(pred[256]{0:T(512)(128)(4,1)S(1)} %get-tuple-element.133) | copy-start | bytes 772
  223.4 249.1 %all-gather.5.cloned.1.call-start = ((), (), s32[]{:S(2)}) async-start(), calls=%async_computation.11 | async-start | bytes 8650752 | tf_op jit(solution)/shard_map/all_gather | solution.py:56
  265.0 152.9 %all-to-all-start.1 = ((bf16[8,3,440,256]{3,2,1,0:T(8,128)(2,1)}), bf16[8,3,440,256]{3,2,1,0:T(8,128)(2,1)}, u32[]{:S(2)}, u32[]{:S(2)}) async-start(bf16[8,3,440,256]{3,2,1,0:T(8,128)(2,1)} %pad_maximum_fusion.1), calls=%async_computation.2 | async-start | bytes 10813440 | tf_op jit(solution)/shard_map/all_to_all | solution.py:64
  270.5 402.8 %reduce-scatter.13.cloned.1.call-start = ((), (), s32[]{:S(2)}) async-start(), calls=%async_computation.15 | async-start | bytes 8650752 | tf_op jit(solution)/shard_map/reduce_scatter | solution.py:60
  502.2 10.8 copy-start.37
  524.3 295.8 %reduce-scatter.9.cloned.1.call-start = ((), (), s32[]{:S(2)}) async-start(), calls=%async_computation.13 | async-start | bytes 9437184 | tf_op jit(solution)/shard_map/reduce_scatter | solution.py:207
  534.4 285.8 %all-gather.9.cloned.1.call-start = ((), (), s32[]{:S(2)}) async-start(), calls=%async_computation.16 | async-start | bytes 1310720 | tf_op jit(solution)/shard_map/all_gather | solution.py:240
  676.4 427.4 %reduce-scatter.11.cloned.1.call-start = ((), (), s32[]{:S(2)}) async-start(), calls=%async_computation.14 | async-start | bytes 1310720 | tf_op jit(solution)/shard_map/reduce_scatter | solution.py:208
  820.1 285.6 %reduce-scatter.15.cloned.1.call-start = ((), (), s32[]{:S(2)}) async-start(), calls=%async_computation.17 | async-start | bytes 2621440 | tf_op jit(solution)/shard_map/reduce_scatter | solution.py:270
  841.2 315.8 %reduce-scatter.17.cloned.1.call-start = ((), (), s32[]{:S(2)}) async-start(), calls=%async_computation.18 | async-start | bytes 9437184 | tf_op jit(solution)/shard_map/reduce_scatter | solution.py:266
  884.6 190.2 %all-to-all-start.3 = ((bf16[8,3,440,256]{3,2,1,0:T(8,128)(2,1)}), bf16[8,3,440,256]{3,2,1,0:T(8,128)(2,1)}, u32[]{:S(2)}, u32[]{:S(2)}) async-start(bf16[8,3,440,256]{3,2,1,0:T(8,128)(2,1)} %maximum_bitcast_fusion), calls=%async_computation.9 | async-start | bytes 10813440 | tf_op jit(solution)/shard_map/all_to_all | solution.py:64
  1074.7 29.0 %all-to-all-start = ((f32[64,4,512]{2,0,1:T(8,128)}), f32[64,4,512]{2,0,1:T(8,128)S(1)}, u32[]{:S(2)}, u32[]{:S(2)}) async-start(f32[64,4,512]{2,0,1:T(8,128)} %bitcast.197), calls=%async_computation.1 | async-start | bytes 1048576 | tf_op jit(solution)/shard_map/all_to_all | solution.py:294
  1103.8 52.4 %copy-start.32 = (pred[2,128]{1,0:T(4,128)(4,1)S(1)}, pred[2,128]{1,0:T(4,128)(4,1)}, u32[]{:S(2)}) copy-start(pred[2,128]{1,0:T(4,128)(4,1)} %get-tuple-element.132) | copy-start | bytes 772
  1109.6 46.5 %all-to-all-start.2 = ((f32[64,4,512]{2,0,1:T(8,128)}), f32[64,4,512]{2,0,1:T(8,128)S(1)}, u32[]{:S(2)}, u32[]{:S(2)}) async-start(f32[64,4,512]{2,0,1:T(8,128)} %bitcast.196), calls=%async_computation.7 | async-start | bytes 1048576 | tf_op jit(solution)/shard_map/all_to_all | solution.py:294
  (30 other events, 137.7 us)
Sparse Core Ops, SparseCore 0:
  220.3 28.4 reduce-scatter.6
  676.5 12.5 all-gather.8
  820.3 23.9 reduce-scatter.10
  846.6 31.1 reduce-scatter.14
  881.3 253.3 reduce-scatter.16
Sparse Core Ops, SparseCore 1:
  224.2 113.1 all-gather.6
  340.7 131.7 all-gather.4
  524.4 148.8 reduce-scatter.12
  676.9 143.1 reduce-scatter.8
